TPU v7x, 32 devices: a whole 2x2x4 slice. The times are simulated.
32 devices in a mesh: gx: 2 (over core), gy: 4 (over y, x), gz: 4 (over z).
Axes of the slice: x: 2, y: 2, z: 4, core: 2. Of those that a mesh axis runs over, the one named last changes fastest.
Arguments:
- queries: bfloat16 [128, 32, 128], P(None, 'gy'), may hold values from -6 to 6
- passages: bfloat16 [1024, 256, 128], P('gx', 'gz'), may hold values from -0.5 to 0.5
- passage_len: int32 [1024], P('gx'), may hold values from 32 to 256
- query_len: int32 [128], replicated, may hold values from 8 to 32
Outputs:
- log_probs: float32 [128, 1024], P(None, ('gx', 'gz'))
All inputs are finite; a program needn't handle non-finite values.
Results may differ from a plain program's by a relative error of at most 0.0003.
Values sent between devices are 32-bit elements; how exact they have to be, the bound alone decides.
No kernel may reach another device: no remote copies, remote signals or barrier semaphores. Data moves between devices by JAX's collectives and lax.ppermute only.
A program may use at most 64 MiB of HBM per device.

v0:
```python
import functools

import jax
import jax.numpy as jnp
from jax import lax
from jax.experimental import pallas as pl
from jax.experimental.pallas import tpu as pltpu
from jax.sharding import PartitionSpec as P


masked_low = -1e30
mebibyte = 2**20


def best_tokens(len_ref, queries_ref, passages_ref, out_ref, first_len, first, place, per_dot, columns):
    _, token_count, width = passages_ref.shape
    query_rows = out_ref.shape[1]
    hidden = lax.axis_index("gz") * token_count
    token_ids = lax.broadcasted_iota(jnp.int32, (token_count, columns), 0)
    tile = passages_ref[first : first + per_dot].reshape(per_dot * token_count, width)
    for j in range(query_rows // columns):
        scores = lax.dot_general(
            tile,
            queries_ref[j * columns : (j + 1) * columns],
            (((1,), (1,)), ((), ())),
            preferred_element_type=jnp.float32,
        )
        best = []
        for k in range(per_dot):
            usable = token_ids < len_ref[first_len + k] - hidden
            mine = jnp.where(usable, scores[k * token_count : (k + 1) * token_count], masked_low)
            best.append(jnp.max(mine, axis=0, keepdims=True))
        out_ref[place : place + per_dot, j * columns : (j + 1) * columns] = jnp.concatenate(best, axis=0)


def block_copies(passages_hbm, block_ref, sems, distance, per_copy):
    block_size = block_ref.shape[0]
    first = (lax.axis_index("gz") ^ distance) * block_size
    return [
        pltpu.make_async_copy(
            passages_hbm.at[pl.ds(first + place, per_copy)],
            block_ref.at[pl.ds(place, per_copy)],
            sems.at[place // per_copy],
        )
        for place in range(0, block_size, per_copy)
    ]


def start_all(passages_hbm, block_ref, sems, distance, per_copy):
    block_size = block_ref.shape[0]
    first = (lax.axis_index("gz") ^ distance) * block_size

    @pl.loop(0, block_size // per_copy)
    def _(m):
        place = m * per_copy
        pltpu.make_async_copy(
            passages_hbm.at[pl.ds(first + place, per_copy)],
            block_ref.at[pl.ds(place, per_copy)],
            sems.at[m],
        ).start()


def first_kernel(
    len_hbm, queries_hbm, passages_hbm, out_ref, len_ref, queries_ref, block_ref, own_sems, sems,
    *, distance, per_dot, columns
):
    own = [
        pltpu.make_async_copy(queries_hbm, queries_ref, own_sems.at[0]),
        pltpu.make_async_copy(len_hbm, len_ref, own_sems.at[1]),
    ]
    copies = block_copies(passages_hbm, block_ref, sems, distance, per_dot)
    done = out_ref.shape[0] // per_dot
    for copy in own + copies[:done]:
        copy.start()
    for copy in own:
        copy.wait()
    first_len = (lax.axis_index("gz") ^ distance) * block_ref.shape[0]
    for m in range(done):
        copies[m].wait()
        if m == 0:
            for copy in copies[done:]:
                copy.start()
        place = m * per_dot
        best_tokens(
            len_ref, queries_ref, block_ref, out_ref, first_len + place, place, place, per_dot, columns
        )
    for copy in copies[done:]:
        copy.wait()


def maxima_kernel(*refs, distance, offset, ahead, per_dot, columns):
    if ahead is None:
        len_ref, queries_ref, block_ref, out_ref = refs
        copies = []
    else:
        len_ref, queries_ref, block_ref, passages_hbm, out_ref, ahead_ref, sems = refs
        copies = block_copies(passages_hbm, ahead_ref, sems, ahead, per_dot)
        start_all(passages_hbm, ahead_ref, sems, ahead, per_dot)
    first_len = (lax.axis_index("gz") ^ distance) * block_ref.shape[0] + offset
    for place in range(0, out_ref.shape[0], per_dot):
        best_tokens(
            len_ref, queries_ref, block_ref, out_ref, first_len + place, offset + place, place, per_dot, columns
        )
    for copy in copies:
        copy.wait()


class Scorer:
    def __init__(self, queries, passages, passage_len, owners):
        self.arguments = [
            pltpu.with_memory_space_constraint(x, pltpu.HBM) for x in (passage_len, queries, passages)
        ]
        passage_count, self.token_count, self.width = passages.shape
        self.query_rows = queries.shape[0]
        self.block_shape = (passage_count // owners, self.token_count, self.width)
        self.block_type = jax.ShapeDtypeStruct(self.block_shape, passages.dtype)
        self.on_chip = {}

    def settings(self, distance, offset, size):
        per_dot = min(16, max(1, 1024 // self.token_count))
        while size % per_dot or self.block_shape[0] % per_dot:
            per_dot //= 2
        fixed = dict(
            out_specs=pl.BlockSpec(memory_space=pltpu.VMEM),
            cost_estimate=pl.CostEstimate(
                flops=4 * size * self.token_count * self.query_rows * self.width,
                bytes_accessed=size * (self.token_count * self.width * 2 + self.query_rows * 4),
                transcendentals=0,
            ),
            compiler_params=pltpu.CompilerParams(vmem_limit_bytes=12 * mebibyte),
            name=f"maxima_{distance}_{offset}",
        )
        result = jax.ShapeDtypeStruct((size, self.query_rows), jnp.float32)
        return per_dot, min(256, self.query_rows), fixed, result

    def first(self, distance, size):
        per_dot, columns, fixed, result = self.settings(distance, 0, size)
        vmem = fixed.pop("out_specs")
        lengths, queries, _ = self.arguments
        start, self.lengths, self.queries, block = pl.pallas_call(
            functools.partial(first_kernel, distance=distance, per_dot=per_dot, columns=columns),
            in_specs=[pl.BlockSpec(memory_space=pltpu.HBM)] * 3,
            out_specs=[vmem, pl.BlockSpec(memory_space=pltpu.SMEM), vmem, vmem],
            out_shape=[
                result,
                jax.ShapeDtypeStruct(lengths.shape, lengths.dtype),
                jax.ShapeDtypeStruct(queries.shape, queries.dtype),
                self.block_type,
            ],
            scratch_shapes=[
                pltpu.SemaphoreType.DMA((2,)),
                pltpu.SemaphoreType.DMA((self.block_shape[0] // per_dot,)),
            ],
            **fixed,
        )(*self.arguments)
        self.queries = pltpu.with_memory_space_constraint(self.queries, pltpu.VMEM)
        self.on_chip[distance] = pltpu.with_memory_space_constraint(block, pltpu.VMEM)
        return start

    def __call__(self, distance, offset, size, ahead=None):
        per_dot, columns, fixed, result = self.settings(distance, offset, size)
        vmem = fixed.pop("out_specs")
        in_specs = [pl.BlockSpec(memory_space=pltpu.SMEM), vmem, vmem]
        operands = [self.lengths, self.queries, self.on_chip[distance]]
        out_specs, out_shape, scratch = [vmem], [result], []
        if ahead is not None:
            in_specs.append(pl.BlockSpec(memory_space=pltpu.HBM))
            operands.append(self.arguments[2])
            out_specs.append(vmem)
            out_shape.append(self.block_type)
            scratch = [pltpu.SemaphoreType.DMA((self.block_shape[0] // per_dot,))]
        maxima, *block = pl.pallas_call(
            functools.partial(
                maxima_kernel,
                distance=distance,
                offset=offset,
                ahead=ahead,
                per_dot=per_dot,
                columns=columns,
            ),
            in_specs=in_specs,
            out_specs=out_specs,
            out_shape=out_shape,
            scratch_shapes=scratch,
            **fixed,
        )(*operands)
        if block:
            self.on_chip[ahead] = pltpu.with_memory_space_constraint(block[0], pltpu.VMEM)
        return maxima


def merge_kernel(*refs, offsets):
    *part_refs, len_ref, out_ref = refs
    size, query_count = out_ref.shape
    lanes = part_refs[0].shape[1]
    query_rows = lanes // query_count
    merged = functools.reduce(
        jnp.maximum, [part[offset : offset + size] for part, offset in zip(part_refs, offsets)]
    )
    shape = (lanes, query_count)
    row = lax.broadcasted_iota(jnp.int32, shape, 0)
    start = lax.broadcasted_iota(jnp.int32, shape, 1) * query_rows
    used = jnp.clip(len_ref[...] - lax.axis_index("gy") * query_rows, 0, query_rows)
    counted = jnp.where((row >= start) & (row < start + used), 1.0, 0.0).astype(jnp.bfloat16)
    total = None
    for _ in range(3):
        piece = merged.astype(jnp.bfloat16)
        merged = merged - piece.astype(jnp.float32)
        term = jnp.dot(piece, counted, preferred_element_type=jnp.float32)
        total = term if total is None else total + term
    out_ref[...] = total


def merge(parts, offsets, size, query_len):
    query_count = query_len.shape[0]
    return pl.pallas_call(
        functools.partial(merge_kernel, offsets=offsets),
        out_shape=jax.ShapeDtypeStruct((size, query_count), jnp.float32),
        compiler_params=pltpu.CompilerParams(vmem_limit_bytes=12 * mebibyte),
    )(*parts, query_len.reshape(1, query_count))


def exchange(array, axis, distance):
    size = lax.axis_size(axis)
    return lax.ppermute(array, axis, [(k, k ^ distance) for k in range(size)])


def hypercube(array, axis, combine):
    distance = 1
    while distance < lax.axis_size(axis):
        array = combine(array, exchange(array, axis, distance))
        distance *= 2
    return array


def join_pairs(one, other):
    top = jnp.maximum(one[0], other[0])
    summed = one[1] * jnp.exp(one[0] - top) + other[1] * jnp.exp(other[0] - top)
    return jnp.stack([top, summed])


def summed_scores(scorer, query_len, owners):
    block_size = scorer.block_shape[0]
    if owners != 4:
        sent = scorer.first(owners - 1, block_size)
        parts = []
        for distance in range(owners - 1, -1, -1):
            ahead = distance - 1 if distance > 0 else None
            if distance < owners - 1:
                sent = scorer(distance, 0, block_size, ahead)
            elif ahead is not None:
                scorer(distance, 0, block_size, ahead)
            parts.append(exchange(sent, "gz", distance) if distance else sent)
        total = merge(parts, [0] * len(parts), block_size, query_len)
        return hypercube(total, "gy", jnp.add)
    early = block_size * 3 // 8
    late = block_size - early
    near_0 = exchange(scorer.first(3, early), "gz", 1)
    near_1 = exchange(scorer(3, early, late, 2), "gz", 1)
    far_0 = exchange(jnp.maximum(scorer(2, 0, early, 1), near_0), "gz", 2)
    beside_0 = exchange(scorer(1, 0, early, 0), "gz", 1)
    far_1 = exchange(jnp.maximum(scorer(2, early, late), near_1), "gz", 2)
    beside_1 = exchange(scorer(1, early, late), "gz", 1)
    own = scorer(0, 0, block_size)
    first = merge([own, beside_0, far_0], [0, 0, 0], early, query_len)
    first = hypercube(first, "gy", jnp.add)
    second = merge([own, beside_1, far_1], [early, 0, 0], late, query_len)
    others = [exchange(second, "gy", distance) for distance in range(1, lax.axis_size("gy"))]
    second = functools.reduce(jnp.add, others, second)
    return jnp.concatenate([first, second])


def shards(queries, passages, passage_len, query_len):
    query_count, query_rows, width = queries.shape
    owners = lax.axis_size("gz")
    flat_queries = queries.reshape(query_count * query_rows, width)
    scorer = Scorer(flat_queries, passages, passage_len, owners)
    scores = summed_scores(scorer, query_len, owners)
    top = jnp.max(scores, axis=0)
    summed = jnp.sum(jnp.exp(scores - top[None]), axis=0)
    pair = hypercube(jnp.stack([top, summed]), "gx", join_pairs)
    others = [exchange(pair, "gz", distance) for distance in range(1, owners)]
    pair = functools.reduce(join_pairs, others, pair)
    return jnp.transpose(scores - (pair[0] + jnp.log(pair[1]))[None])


def solution(mesh):
    return jax.shard_map(
        shards,
        mesh=mesh,
        in_specs=(P(None, "gy", None), P("gx", "gz", None), P("gx"), P()),
        out_specs=P(None, ("gx", "gz")),
        check_vma=False,
    )
```

profile of v0, /device:TPU:0, one launch (start us, length us, event | category | flops | bytes accessed | tf_op | source)
XLA Modules:
  0.0 69.7 jit_solution(17233018856865682602)
XLA Ops:
  0.0 3.9 %maxima_3_0.1 = (f32[48,1024]{1,0:T(8,128)S(1)}, s32[512]{0:T(512)S(1)}, bf16[1024,128]{1,0:T(8,128)(2,1)S(1)}, bf16[128,64,128]{2,1,0:T(8,128)(2,1)S(1)}) custom-call(s32[512]{0:T(512)} %len_hbm.1, bf16[1024,128]{1,0:T(8,128)(2,1)} %bitcast.14, bf16[512,64,128]{2,1,0:T(8,128)(2,1)} %refs_3_.5), custom_call_target="tpu_custom_call" | custom-call | flops 1610612736 | bytes 983040 | tf_op jit(solution)/shard_map/maxima_3_0/pallas_call | solution.py:140
  3.9 3.1 %collective-permute-start.1 = (f32[48,1024]{1,0:T(8,128)S(1)}, f32[48,1024]{1,0:T(8,128)S(1)}, u32[]{:S(2)}, u32[]{:S(2)}) collective-permute-start(f32[48,1024]{1,0:T(8,128)S(1)} %get-tuple-element.23), channel_id=1, source_target_pairs={{0,1},{1,0},{2,3},{3,2},{4,5},{5,4},{6,7},{7,6},{8,9},{9,8},{10,11... | collective-permute-start | bytes 589832 | tf_op jit(solution)/shard_map/ppermute | solution.py:225
  7.0 3.6 %maxima_3_48.1 = (f32[80,1024]{1,0:T(8,128)S(1)}, bf16[128,64,128]{2,1,0:T(8,128)(2,1)S(1)}) custom-call(s32[512]{0:T(512)S(1)} %get-tuple-element.15.refs_0_, bf16[1024,128]{1,0:T(8,128)(2,1)S(1)} %get-tuple-element.16.refs_1_, bf16[128,64,128]{2,1,0:T(8,128)(2,1)S(1)} %get-tuple-element.17.refs_2_, bf16[512,64,128]{2,1,0:T(8,128)(2,1)} %refs_3_.5), custom_call_target="tpu_custom_call" | custom-call | flops 2684354560 | bytes 1638400 | tf_op jit(solution)/shard_map/maxima_3_48/pallas_call | solution.py:172
  10.7 2.5 %maxima_2_0.1 = (f32[48,1024]{1,0:T(8,128)S(1)}, bf16[128,64,128]{2,1,0:T(8,128)(2,1)S(1)}) custom-call(s32[512]{0:T(512)S(1)} %get-tuple-element.15.refs_0_, bf16[1024,128]{1,0:T(8,128)(2,1)S(1)} %get-tuple-element.16.refs_1_, bf16[128,64,128]{2,1,0:T(8,128)(2,1)S(1)} %get-tuple-element.18.refs_2_, bf16[512,64,128]{2,1,0:T(8,128)(2,1)} %refs_3_.5), custom_call_target="tpu_custom_call" | custom-call | flops 1610612736 | bytes 983040 | tf_op jit(solution)/shard_map/maxima_2_0/pallas_call | solution.py:172
  13.2 2.7 %maxima_1_0.1 = (f32[48,1024]{1,0:T(8,128)S(1)}, bf16[128,64,128]{2,1,0:T(8,128)(2,1)S(1)}) custom-call(s32[512]{0:T(512)S(1)} %get-tuple-element.15.refs_0_, bf16[1024,128]{1,0:T(8,128)(2,1)S(1)} %get-tuple-element.16.refs_1_, bf16[128,64,128]{2,1,0:T(8,128)(2,1)S(1)} %get-tuple-element.19.refs_2_, bf16[512,64,128]{2,1,0:T(8,128)(2,1)} %refs_3_.5), custom_call_target="tpu_custom_call" | custom-call | flops 1610612736 | bytes 983040 | tf_op jit(solution)/shard_map/maxima_1_0/pallas_call | solution.py:172
  15.9 0.1 collective-permute-start
  16.0 2.0 %collective-permute-start.6 = (f32[80,1024]{1,0:T(8,128)S(1)}, f32[80,1024]{1,0:T(8,128)S(1)}, u32[]{:S(2)}, u32[]{:S(2)}) collective-permute-start(f32[80,1024]{1,0:T(8,128)S(1)} %get-tuple-element.24), channel_id=1, source_target_pairs={{0,1},{1,0},{2,3},{3,2},{4,5},{5,4},{6,7},{7,6},{8,9},{9,8},{10,11... | collective-permute-start | bytes 983048 | tf_op jit(solution)/shard_map/ppermute | solution.py:225
  18.0 3.5 %maxima_1_48.1 = f32[80,1024]{1,0:T(8,128)S(1)} custom-call(s32[512]{0:T(512)S(1)} %get-tuple-element.15.refs_0_, bf16[1024,128]{1,0:T(8,128)(2,1)S(1)} %get-tuple-element.16.refs_1_, bf16[128,64,128]{2,1,0:T(8,128)(2,1)S(1)} %get-tuple-element.19.refs_2_), custom_call_target="tpu_custom_call" | custom-call | flops 2684354560 | bytes 1638400 | tf_op jit(solution)/shard_map/maxima_1_48/pallas_call | solution.py:172
  21.5 0.1 collective-permute-start.5
  21.6 3.5 %maxima_2_48.1 = f32[80,1024]{1,0:T(8,128)S(1)} custom-call(s32[512]{0:T(512)S(1)} %get-tuple-element.15.refs_0_, bf16[1024,128]{1,0:T(8,128)(2,1)S(1)} %get-tuple-element.16.refs_1_, bf16[128,64,128]{2,1,0:T(8,128)(2,1)S(1)} %get-tuple-element.18.refs_2_), custom_call_target="tpu_custom_call" | custom-call | flops 2684354560 | bytes 1638400 | tf_op jit(solution)/shard_map/maxima_2_48/pallas_call | solution.py:172
  25.1 0.0 collective-permute-done.1
  25.2 3.0 %collective-permute-start.2 = (f32[48,1024]{1,0:T(8,128)S(1)}, f32[48,1024]{1,0:T(8,128)S(1)}, u32[]{:S(2)}, u32[]{:S(2)}) collective-permute-start(f32[48,1024]{1,0:T(8,128)S(1)} %max.24), channel_id=1, source_target_pairs={{0,2},{1,3},{2,0},{3,1},{4,6},{5,7},{6,4},{7,5},{8,10},{9,11},{10,... | collective-permute-start | bytes 589832 | tf_op jit(solution)/shard_map/ppermute | solution.py:225
  28.2 6.8 %collective-permute-done.6 = f32[80,1024]{1,0:T(8,128)S(1)} collective-permute-done((f32[80,1024]{1,0:T(8,128)S(1)}, f32[80,1024]{1,0:T(8,128)S(1)}, u32[]{:S(2)}, u32[]{:S(2)}) %collective-permute-start.6) | collective-permute-done | bytes 327712 | tf_op jit(solution)/shard_map/ppermute | solution.py:225
  35.1 3.3 %collective-permute-start.7 = (f32[80,1024]{1,0:T(8,128)S(1)}, f32[80,1024]{1,0:T(8,128)S(1)}, u32[]{:S(2)}, u32[]{:S(2)}) collective-permute-start(f32[80,1024]{1,0:T(8,128)S(1)} %max.25), channel_id=1, source_target_pairs={{0,2},{1,3},{2,0},{3,1},{4,6},{5,7},{6,4},{7,5},{8,10},{9,11},{10,... | collective-permute-start | bytes 983048 | tf_op jit(solution)/shard_map/ppermute | solution.py:225
  38.4 0.0 copy-start
  38.4 5.1 %maxima_0_0.1.refs_0_ = f32[128,1024]{1,0:T(8,128)S(1)} custom-call(s32[512]{0:T(512)S(1)} %get-tuple-element.15.refs_0_, bf16[1024,128]{1,0:T(8,128)(2,1)S(1)} %get-tuple-element.16.refs_1_, bf16[128,64,128]{2,1,0:T(8,128)(2,1)S(1)} %get-tuple-element.20.refs_2_), custom_call_target="tpu_custom_call" | custom-call | flops 4294967296 | bytes 2621440 | tf_op jit(solution)/shard_map/maxima_0_0/pallas_call | solution.py:172
  43.5 0.0 collective-permute-done.refs_1_
  43.5 0.0 collective-permute-done.2.refs_2_
  43.5 0.0 copy-done
  43.5 0.3 shard_map.46
  43.9 1.6 %collective-permute-start.3 = (f32[48,128]{1,0:T(8,128)S(1)}, f32[48,128]{1,0:T(8,128)S(1)}, u32[]{:S(2)}, u32[]{:S(2)}) collective-permute-start(f32[48,128]{1,0:T(8,128)S(1)} %shard_map.46), channel_id=1, source_target_pairs={{0,4},{4,0},{8,12},{12,8},{1,5},{5,1},{9,13},{13,9},{2,6},{6,2},{1... | collective-permute-start | bytes 73736 | tf_op jit(solution)/shard_map/ppermute | solution.py:225
  45.4 2.3 %collective-permute-done.3 = f32[48,128]{1,0:T(8,128)S(1)} collective-permute-done((f32[48,128]{1,0:T(8,128)S(1)}, f32[48,128]{1,0:T(8,128)S(1)}, u32[]{:S(2)}, u32[]{:S(2)}) %collective-permute-start.3) | collective-permute-done | bytes 24608 | tf_op jit(solution)/shard_map/ppermute | solution.py:225
  47.8 1.8 %collective-permute-start.4 = (f32[48,128]{1,0:T(8,128)S(1)}, f32[48,128]{1,0:T(8,128)S(1)}, u32[]{:S(2)}, u32[]{:S(2)}) collective-permute-start(f32[48,128]{1,0:T(8,128)S(1)} %add.36), channel_id=1, source_target_pairs={{0,8},{4,12},{8,0},{12,4},{1,9},{5,13},{9,1},{13,5},{2,10},{6,14},... | collective-permute-start | bytes 73736 | tf_op jit(solution)/shard_map/ppermute | solution.py:225
  49.6 0.0 collective-permute-done.5.refs_1_
  49.6 4.6 %collective-permute-done.7.refs_2_ = f32[80,1024]{1,0:T(8,128)S(1)} collective-permute-done((f32[80,1024]{1,0:T(8,128)S(1)}, f32[80,1024]{1,0:T(8,128)S(1)}, u32[]{:S(2)}, u32[]{:S(2)}) %collective-permute-start.7) | collective-permute-done | bytes 327712 | tf_op jit(solution)/shard_map/ppermute | solution.py:225
  54.2 0.4 shard_map.47
  54.6 2.5 %collective-permute-start.10 = (f32[80,128]{1,0:T(8,128)S(1)}, f32[80,128]{1,0:T(8,128)S(1)}, u32[]{:S(2)}, u32[]{:S(2)}) collective-permute-start(f32[80,128]{1,0:T(8,128)S(1)} %shard_map.47), channel_id=1, source_target_pairs={{0,12},{4,8},{8,4},{12,0},{1,13},{5,9},{9,5},{13,1},{2,14},{6,10},... | collective-permute-start | bytes 122888 | tf_op jit(solution)/shard_map/ppermute | solution.py:225
  57.1 0.5 collective-permute-start.9
  57.6 0.5 collective-permute-start.8
  58.2 0.0 collective-permute-done.4
  58.2 1.4 %collective-permute-done.10 = f32[80,128]{1,0:T(8,128)S(1)} collective-permute-done((f32[80,128]{1,0:T(8,128)S(1)}, f32[80,128]{1,0:T(8,128)S(1)}, u32[]{:S(2)}, u32[]{:S(2)}) %collective-permute-start.10) | collective-permute-done | bytes 40992 | tf_op jit(solution)/shard_map/ppermute | solution.py:225
  59.6 1.6 %collective-permute-done.9 = f32[80,128]{1,0:T(8,128)S(1)} collective-permute-done((f32[80,128]{1,0:T(8,128)S(1)}, f32[80,128]{1,0:T(8,128)S(1)}, u32[]{:S(2)}, u32[]{:S(2)}) %collective-permute-start.9) | collective-permute-done | bytes 40992 | tf_op jit(solution)/shard_map/ppermute | solution.py:225
  61.1 0.5 collective-permute-done.8
  61.7 0.1 collective-permute-start.11
  61.8 1.1 %collective-permute-done.11 = f32[2,128]{1,0:T(2,128)S(1)} collective-permute-done((f32[2,128]{1,0:T(2,128)S(1)}, f32[2,128]{1,0:T(2,128)S(1)}, u32[]{:S(2)}, u32[]{:S(2)}) %collective-permute-start.11) | collective-permute-done | bytes 1056 | tf_op jit(solution)/shard_map/ppermute | solution.py:225
  63.0 0.1 collective-permute-start.14
  63.1 0.1 collective-permute-start.13
  63.1 4.3 %collective-permute-start.12 = (f32[2,128]{1,0:T(2,128)S(1)}, f32[2,128]{1,0:T(2,128)S(1)}, u32[]{:S(2)}, u32[]{:S(2)}) collective-permute-start(f32[2,128]{1,0:T(2,128)S(1)} %pad_maximum_fusion.2), channel_id=1, source_target_pairs={{0,1},{1,0},{2,3},{3,2},{4,5},{5,4},{6,7},{7,6},{8,9},{9,8},{10,11... | collective-permute-start | bytes 3080 | tf_op jit(solution)/shard_map/ppermute | solution.py:225
  67.4 1.0 %collective-permute-done.14 = f32[2,128]{1,0:T(2,128)S(1)} collective-permute-done((f32[2,128]{1,0:T(2,128)S(1)}, f32[2,128]{1,0:T(2,128)S(1)}, u32[]{:S(2)}, u32[]{:S(2)}) %collective-permute-start.14) | collective-permute-done | bytes 1056 | tf_op jit(solution)/shard_map/ppermute | solution.py:225
  68.4 0.0 collective-permute-done.13
  68.4 0.6 collective-permute-done.12
  69.0 0.7 %copy.5 = f32[128,128]{1,0:T(8,128)} copy(f32[128,128]{0,1:T(8,128)S(1)} %subtract_bitcast_fusion) | data formatting | bytes 131072 | tf_op jit(solution)/shard_map/transpose | solution.py:284
  (12 shorter events, 0.2 us)
Async XLA Ops:
  3.9 21.2 %collective-permute-start.1 = (f32[48,1024]{1,0:T(8,128)S(1)}, f32[48,1024]{1,0:T(8,128)S(1)}, u32[]{:S(2)}, u32[]{:S(2)}) collective-permute-start(f32[48,1024]{1,0:T(8,128)S(1)} %get-tuple-element.23), channel_id=1, source_target_pairs={{0,1},{1,0},{2,3},{3,2},{4,5},{5,4},{6,7},{7,6},{8,9},{9,8},{10,11... | collective-permute-start | bytes 589832 | tf_op jit(solution)/shard_map/ppermute | solution.py:225
  15.9 27.6 %collective-permute-start = (f32[48,1024]{1,0:T(8,128)S(1)}, f32[48,1024]{1,0:T(8,128)S(1)}, u32[]{:S(2)}, u32[]{:S(2)}) collective-permute-start(f32[48,1024]{1,0:T(8,128)S(1)} %get-tuple-element.21), channel_id=1, source_target_pairs={{0,1},{1,0},{2,3},{3,2},{4,5},{5,4},{6,7},{7,6},{8,9},{9,8},{10,11... | collective-permute-start | bytes 589832 | tf_op jit(solution)/shard_map/ppermute | solution.py:225
  16.0 19.0 %collective-permute-start.6 = (f32[80,1024]{1,0:T(8,128)S(1)}, f32[80,1024]{1,0:T(8,128)S(1)}, u32[]{:S(2)}, u32[]{:S(2)}) collective-permute-start(f32[80,1024]{1,0:T(8,128)S(1)} %get-tuple-element.24), channel_id=1, source_target_pairs={{0,1},{1,0},{2,3},{3,2},{4,5},{5,4},{6,7},{7,6},{8,9},{9,8},{10,11... | collective-permute-start | bytes 983048 | tf_op jit(solution)/shard_map/ppermute | solution.py:225
  21.5 28.1 %collective-permute-start.5 = (f32[80,1024]{1,0:T(8,128)S(1)}, f32[80,1024]{1,0:T(8,128)S(1)}, u32[]{:S(2)}, u32[]{:S(2)}) collective-permute-start(f32[80,1024]{1,0:T(8,128)S(1)} %maxima_1_48.1), channel_id=1, source_target_pairs={{0,1},{1,0},{2,3},{3,2},{4,5},{5,4},{6,7},{7,6},{8,9},{9,8},{10,11... | collective-permute-start | bytes 983048 | tf_op jit(solution)/shard_map/ppermute | solution.py:225
  25.2 18.3 %collective-permute-start.2 = (f32[48,1024]{1,0:T(8,128)S(1)}, f32[48,1024]{1,0:T(8,128)S(1)}, u32[]{:S(2)}, u32[]{:S(2)}) collective-permute-start(f32[48,1024]{1,0:T(8,128)S(1)} %max.24), channel_id=1, source_target_pairs={{0,2},{1,3},{2,0},{3,1},{4,6},{5,7},{6,4},{7,5},{8,10},{9,11},{10,... | collective-permute-start | bytes 589832 | tf_op jit(solution)/shard_map/ppermute | solution.py:225
  35.1 19.1 %collective-permute-start.7 = (f32[80,1024]{1,0:T(8,128)S(1)}, f32[80,1024]{1,0:T(8,128)S(1)}, u32[]{:S(2)}, u32[]{:S(2)}) collective-permute-start(f32[80,1024]{1,0:T(8,128)S(1)} %max.25), channel_id=1, source_target_pairs={{0,2},{1,3},{2,0},{3,1},{4,6},{5,7},{6,4},{7,5},{8,10},{9,11},{10,... | collective-permute-start | bytes 983048 | tf_op jit(solution)/shard_map/ppermute | solution.py:225
  38.4 5.1 %copy-start = (s32[128]{0:T(128)S(1)}, s32[128]{0:T(128)}, u32[]{:S(2)}) copy-start(s32[128]{0:T(128)} %param.7) | copy-start | bytes 1540
  43.9 3.9 %collective-permute-start.3 = (f32[48,128]{1,0:T(8,128)S(1)}, f32[48,128]{1,0:T(8,128)S(1)}, u32[]{:S(2)}, u32[]{:S(2)}) collective-permute-start(f32[48,128]{1,0:T(8,128)S(1)} %shard_map.46), channel_id=1, source_target_pairs={{0,4},{4,0},{8,12},{12,8},{1,5},{5,1},{9,13},{13,9},{2,6},{6,2},{1... | collective-permute-start | bytes 73736 | tf_op jit(solution)/shard_map/ppermute | solution.py:225
  47.8 10.4 %collective-permute-start.4 = (f32[48,128]{1,0:T(8,128)S(1)}, f32[48,128]{1,0:T(8,128)S(1)}, u32[]{:S(2)}, u32[]{:S(2)}) collective-permute-start(f32[48,128]{1,0:T(8,128)S(1)} %add.36), channel_id=1, source_target_pairs={{0,8},{4,12},{8,0},{12,4},{1,9},{5,13},{9,1},{13,5},{2,10},{6,14},... | collective-permute-start | bytes 73736 | tf_op jit(solution)/shard_map/ppermute | solution.py:225
  54.6 5.0 %collective-permute-start.10 = (f32[80,128]{1,0:T(8,128)S(1)}, f32[80,128]{1,0:T(8,128)S(1)}, u32[]{:S(2)}, u32[]{:S(2)}) collective-permute-start(f32[80,128]{1,0:T(8,128)S(1)} %shard_map.47), channel_id=1, source_target_pairs={{0,12},{4,8},{8,4},{12,0},{1,13},{5,9},{9,5},{13,1},{2,14},{6,10},... | collective-permute-start | bytes 122888 | tf_op jit(solution)/shard_map/ppermute | solution.py:225
  57.1 4.0 %collective-permute-start.9 = (f32[80,128]{1,0:T(8,128)S(1)}, f32[80,128]{1,0:T(8,128)S(1)}, u32[]{:S(2)}, u32[]{:S(2)}) collective-permute-start(f32[80,128]{1,0:T(8,128)S(1)} %shard_map.47), channel_id=1, source_target_pairs={{0,8},{4,12},{8,0},{12,4},{1,9},{5,13},{9,1},{13,5},{2,10},{6,14},... | collective-permute-start | bytes 122888 | tf_op jit(solution)/shard_map/ppermute | solution.py:225
  57.6 4.0 %collective-permute-start.8 = (f32[80,128]{1,0:T(8,128)S(1)}, f32[80,128]{1,0:T(8,128)S(1)}, u32[]{:S(2)}, u32[]{:S(2)}) collective-permute-start(f32[80,128]{1,0:T(8,128)S(1)} %shard_map.47), channel_id=1, source_target_pairs={{0,4},{4,0},{8,12},{12,8},{1,5},{5,1},{9,13},{13,9},{2,6},{6,2},{1... | collective-permute-start | bytes 122888 | tf_op jit(solution)/shard_map/ppermute | solution.py:225
  61.7 1.2 %collective-permute-start.11 = (f32[2,128]{1,0:T(2,128)S(1)}, f32[2,128]{1,0:T(2,128)S(1)}, u32[]{:S(2)}, u32[]{:S(2)}) collective-permute-start(f32[2,128]{1,0:T(2,128)S(1)} %pad_maximum_fusion.1), channel_id=1, source_target_pairs={{0,16},{16,0},{1,17},{17,1},{2,18},{18,2},{3,19},{19,3},{4,20},{20... | collective-permute-start | bytes 3080 | tf_op jit(solution)/shard_map/ppermute | solution.py:225
  63.0 5.4 %collective-permute-start.14 = (f32[2,128]{1,0:T(2,128)S(1)}, f32[2,128]{1,0:T(2,128)S(1)}, u32[]{:S(2)}, u32[]{:S(2)}) collective-permute-start(f32[2,128]{1,0:T(2,128)S(1)} %pad_maximum_fusion.2), channel_id=1, source_target_pairs={{0,3},{1,2},{2,1},{3,0},{4,7},{5,6},{6,5},{7,4},{8,11},{9,10},{10,... | collective-permute-start | bytes 3080 | tf_op jit(solution)/shard_map/ppermute | solution.py:225
  63.1 5.4 %collective-permute-start.13 = (f32[2,128]{1,0:T(2,128)S(1)}, f32[2,128]{1,0:T(2,128)S(1)}, u32[]{:S(2)}, u32[]{:S(2)}) collective-permute-start(f32[2,128]{1,0:T(2,128)S(1)} %pad_maximum_fusion.2), channel_id=1, source_target_pairs={{0,2},{1,3},{2,0},{3,1},{4,6},{5,7},{6,4},{7,5},{8,10},{9,11},{10,... | collective-permute-start | bytes 3080 | tf_op jit(solution)/shard_map/ppermute | solution.py:225
  63.1 5.8 %collective-permute-start.12 = (f32[2,128]{1,0:T(2,128)S(1)}, f32[2,128]{1,0:T(2,128)S(1)}, u32[]{:S(2)}, u32[]{:S(2)}) collective-permute-start(f32[2,128]{1,0:T(2,128)S(1)} %pad_maximum_fusion.2), channel_id=1, source_target_pairs={{0,1},{1,0},{2,3},{3,2},{4,5},{5,4},{6,7},{7,6},{8,9},{9,8},{10,11... | collective-permute-start | bytes 3080 | tf_op jit(solution)/shard_map/ppermute | solution.py:225
where the time goes:
time: 69.9 us; the launch traced here: 69.7 us
  Pallas kernels  25.6 us (37%)
  starting transfers between devices  23.1 us (33%)
  waiting for transfers between devices  19.9 us (28%)
  local copies, waits for them, and re-layouts  0.73 us (1%)
    ppermute x15, starting transfers between devices, exchange(): return lax.ppermute(array, axis, [(k, k ^ distance) for k in range(size)])  23.1 us
    pallas_call x6, Pallas kernels, __call__(): pl.pallas_call(functools.partial(maxima_kernel, distance=distance, offset...  20.9 us
    ppermute x15, waiting for transfers between devices, exchange(): return lax.ppermute(array, axis, [(k, k ^ distance) for k in range(size)])  19.9 us
    pallas_call x1, Pallas kernels, first(): pl.pallas_call(functools.partial(first_kernel, distance=distance, per_dot...  3.9 us
  transfers between devices with their start and end apart: 15, of which 9 were waited for; matrix products, arithmetic and copies ran while one was open for 0% of the time, Pallas kernels for 31%

commit v1 on v0

--- a/solution.py
+++ b/solution.py
@@ -261,10 +261,12 @@
     beside_0 = exchange(scorer(1, 0, early, 0), "gz", 1)
     far_1 = exchange(jnp.maximum(scorer(2, early, late), near_1), "gz", 2)
     beside_1 = exchange(scorer(1, early, late), "gz", 1)
-    own = scorer(0, 0, block_size)
-    first = merge([own, beside_0, far_0], [0, 0, 0], early, query_len)
+    own_0 = scorer(0, 0, early)
+    own_1 = scorer(0, early, late)
+    first = merge([own_0, beside_0, far_0], [0, 0, 0], early, query_len)
     first = hypercube(first, "gy", jnp.add)
-    second = merge([own, beside_1, far_1], [early, 0, 0], late, query_len)
+    query_len, first = lax.optimization_barrier((query_len, first))
+    second = merge([own_1, beside_1, far_1], [0, 0, 0], late, query_len)
     others = [exchange(second, "gy", distance) for distance in range(1, lax.axis_size("gy"))]
     second = functools.reduce(jnp.add, others, second)
     return jnp.concatenate([first, second])

time: 69.9 us -> 70.3 us (level)
  starting transfers between devices: 23.1 us -> 21 us
  waiting for transfers between devices: 19.9 us -> 21.5 us
  Pallas kernels: 25.6 us -> 26.5 us
    ppermute x15, starting transfers between devices: 23.1 us -> 21 us  [exchange(): return lax.ppermute(array, axis, [(k, k ^ distance) for k in range(size)])]
    ppermute x15, waiting for transfers between devices: 19.9 us -> 21.5 us  [exchange(): return lax.ppermute(array, axis, [(k, k ^ distance) for k in range(size)])]
    pallas_call x6 -> x7, Pallas kernels: 20.9 us -> 21.9 us  [__call__(): pl.pallas_call(functools.partial(maxima_kernel, distance=distance, offset...]
  transfers between devices with their start and end apart: 15 -> 15, of which waited for: 9 -> 10; matrix products, arithmetic and copies ran while one was open for 0% -> 0% of each run, Pallas kernels for 31% -> 32%
where the time goes in v1:
time: 70.3 us; the launch traced here: 70.1 us
  Pallas kernels  26.5 us (38%)
  waiting for transfers between devices  21.5 us (31%)
  starting transfers between devices  21 us (30%)
  local copies, waits for them, and re-layouts  0.73 us (1%)
    pallas_call x7, Pallas kernels, __call__(): pl.pallas_call(functools.partial(maxima_kernel, distance=distance, offset...  21.9 us
    ppermute x15, waiting for transfers between devices, exchange(): return lax.ppermute(array, axis, [(k, k ^ distance) for k in range(size)])  21.5 us
    ppermute x15, starting transfers between devices, exchange(): return lax.ppermute(array, axis, [(k, k ^ distance) for k in range(size)])  21 us
    pallas_call x1, Pallas kernels, first(): pl.pallas_call(functools.partial(first_kernel, distance=distance, per_dot...  3.9 us
  transfers between devices with their start and end apart: 15, of which 10 were waited for; matrix products, arithmetic and copies ran while one was open for 0% of the time, Pallas kernels for 32%

profile of v1, /device:TPU:0, one launch (start us, length us, event | category | flops | bytes accessed | tf_op | source)
XLA Modules:
  0.0 70.1 jit_solution(6465592054860084332)
XLA Ops:
  0.0 3.9 %maxima_3_0.1 = (f32[48,1024]{1,0:T(8,128)S(1)}, s32[512]{0:T(512)S(1)}, bf16[1024,128]{1,0:T(8,128)(2,1)S(1)}, bf16[128,64,128]{2,1,0:T(8,128)(2,1)S(1)}) custom-call(s32[512]{0:T(512)} %len_hbm.1, bf16[1024,128]{1,0:T(8,128)(2,1)} %bitcast.15, bf16[512,64,128]{2,1,0:T(8,128)(2,1)} %refs_3_.5), custom_call_target="tpu_custom_call" | custom-call | flops 1610612736 | bytes 983040 | tf_op jit(solution)/shard_map/maxima_3_0/pallas_call | solution.py:140
  3.9 3.1 %collective-permute-start.1 = (f32[48,1024]{1,0:T(8,128)S(1)}, f32[48,1024]{1,0:T(8,128)S(1)}, u32[]{:S(2)}, u32[]{:S(2)}) collective-permute-start(f32[48,1024]{1,0:T(8,128)S(1)} %get-tuple-element.25), channel_id=1, source_target_pairs={{0,1},{1,0},{2,3},{3,2},{4,5},{5,4},{6,7},{7,6},{8,9},{9,8},{10,11... | collective-permute-start | bytes 589832 | tf_op jit(solution)/shard_map/ppermute | solution.py:225
  7.0 3.6 %maxima_3_48.1 = (f32[80,1024]{1,0:T(8,128)S(1)}, bf16[128,64,128]{2,1,0:T(8,128)(2,1)S(1)}) custom-call(s32[512]{0:T(512)S(1)} %get-tuple-element.17.refs_0_, bf16[1024,128]{1,0:T(8,128)(2,1)S(1)} %get-tuple-element.18.refs_1_, bf16[128,64,128]{2,1,0:T(8,128)(2,1)S(1)} %get-tuple-element.19.refs_2_, bf16[512,64,128]{2,1,0:T(8,128)(2,1)} %refs_3_.5), custom_call_target="tpu_custom_call" | custom-call | flops 2684354560 | bytes 1638400 | tf_op jit(solution)/shard_map/maxima_3_48/pallas_call | solution.py:172
  10.7 2.5 %maxima_2_0.1 = (f32[48,1024]{1,0:T(8,128)S(1)}, bf16[128,64,128]{2,1,0:T(8,128)(2,1)S(1)}) custom-call(s32[512]{0:T(512)S(1)} %get-tuple-element.17.refs_0_, bf16[1024,128]{1,0:T(8,128)(2,1)S(1)} %get-tuple-element.18.refs_1_, bf16[128,64,128]{2,1,0:T(8,128)(2,1)S(1)} %get-tuple-element.20.refs_2_, bf16[512,64,128]{2,1,0:T(8,128)(2,1)} %refs_3_.5), custom_call_target="tpu_custom_call" | custom-call | flops 1610612736 | bytes 983040 | tf_op jit(solution)/shard_map/maxima_2_0/pallas_call | solution.py:172
  13.2 2.7 %maxima_1_0.1 = (f32[48,1024]{1,0:T(8,128)S(1)}, bf16[128,64,128]{2,1,0:T(8,128)(2,1)S(1)}) custom-call(s32[512]{0:T(512)S(1)} %get-tuple-element.17.refs_0_, bf16[1024,128]{1,0:T(8,128)(2,1)S(1)} %get-tuple-element.18.refs_1_, bf16[128,64,128]{2,1,0:T(8,128)(2,1)S(1)} %get-tuple-element.21.refs_2_, bf16[512,64,128]{2,1,0:T(8,128)(2,1)} %refs_3_.5), custom_call_target="tpu_custom_call" | custom-call | flops 1610612736 | bytes 983040 | tf_op jit(solution)/shard_map/maxima_1_0/pallas_call | solution.py:172
  15.9 0.1 collective-permute-start
  16.0 2.0 %collective-permute-start.6 = (f32[80,1024]{1,0:T(8,128)S(1)}, f32[80,1024]{1,0:T(8,128)S(1)}, u32[]{:S(2)}, u32[]{:S(2)}) collective-permute-start(f32[80,1024]{1,0:T(8,128)S(1)} %get-tuple-element.27), channel_id=1, source_target_pairs={{0,1},{1,0},{2,3},{3,2},{4,5},{5,4},{6,7},{7,6},{8,9},{9,8},{10,11... | collective-permute-start | bytes 983048 | tf_op jit(solution)/shard_map/ppermute | solution.py:225
  18.0 3.5 %maxima_1_48.1 = f32[80,1024]{1,0:T(8,128)S(1)} custom-call(s32[512]{0:T(512)S(1)} %get-tuple-element.17.refs_0_, bf16[1024,128]{1,0:T(8,128)(2,1)S(1)} %get-tuple-element.18.refs_1_, bf16[128,64,128]{2,1,0:T(8,128)(2,1)S(1)} %get-tuple-element.21.refs_2_), custom_call_target="tpu_custom_call" | custom-call | flops 2684354560 | bytes 1638400 | tf_op jit(solution)/shard_map/maxima_1_48/pallas_call | solution.py:172
  21.5 0.1 collective-permute-start.5
  21.6 0.0 collective-permute-done.1
  21.7 3.0 %collective-permute-start.2 = (f32[48,1024]{1,0:T(8,128)S(1)}, f32[48,1024]{1,0:T(8,128)S(1)}, u32[]{:S(2)}, u32[]{:S(2)}) collective-permute-start(f32[48,1024]{1,0:T(8,128)S(1)} %max.24), channel_id=1, source_target_pairs={{0,2},{1,3},{2,0},{3,1},{4,6},{5,7},{6,4},{7,5},{8,10},{9,11},{10,... | collective-permute-start | bytes 589832 | tf_op jit(solution)/shard_map/ppermute | solution.py:225
  24.7 3.5 %maxima_2_48.1 = f32[80,1024]{1,0:T(8,128)S(1)} custom-call(s32[512]{0:T(512)S(1)} %get-tuple-element.17.refs_0_, bf16[1024,128]{1,0:T(8,128)(2,1)S(1)} %get-tuple-element.18.refs_1_, bf16[128,64,128]{2,1,0:T(8,128)(2,1)S(1)} %get-tuple-element.20.refs_2_), custom_call_target="tpu_custom_call" | custom-call | flops 2684354560 | bytes 1638400 | tf_op jit(solution)/shard_map/maxima_2_48/pallas_call | solution.py:172
  28.2 6.8 %collective-permute-done.6 = f32[80,1024]{1,0:T(8,128)S(1)} collective-permute-done((f32[80,1024]{1,0:T(8,128)S(1)}, f32[80,1024]{1,0:T(8,128)S(1)}, u32[]{:S(2)}, u32[]{:S(2)}) %collective-permute-start.6) | collective-permute-done | bytes 327712 | tf_op jit(solution)/shard_map/ppermute | solution.py:225
  35.1 0.6 collective-permute-start.7
  35.7 0.0 copy-start
  35.7 2.4 %maxima_0_0.1.refs_0_ = f32[48,1024]{1,0:T(8,128)S(1)} custom-call(s32[512]{0:T(512)S(1)} %get-tuple-element.17.refs_0_, bf16[1024,128]{1,0:T(8,128)(2,1)S(1)} %get-tuple-element.18.refs_1_, bf16[128,64,128]{2,1,0:T(8,128)(2,1)S(1)} %get-tuple-element.22.refs_2_), custom_call_target="tpu_custom_call" | custom-call | flops 1610612736 | bytes 983040 | tf_op jit(solution)/shard_map/maxima_0_0/pallas_call | solution.py:172
  38.1 0.0 collective-permute-done.refs_1_
  38.1 1.5 %collective-permute-done.2.refs_2_ = f32[48,1024]{1,0:T(8,128)S(1)} collective-permute-done((f32[48,1024]{1,0:T(8,128)S(1)}, f32[48,1024]{1,0:T(8,128)S(1)}, u32[]{:S(2)}, u32[]{:S(2)}) %collective-permute-start.2) | collective-permute-done | bytes 196640 | tf_op jit(solution)/shard_map/ppermute | solution.py:225
  39.6 0.0 copy-done
  39.6 0.3 shard_map.46
  40.0 2.0 %collective-permute-start.3 = (f32[48,128]{1,0:T(8,128)S(1)}, f32[48,128]{1,0:T(8,128)S(1)}, u32[]{:S(2)}, u32[]{:S(2)}) collective-permute-start(f32[48,128]{1,0:T(8,128)S(1)} %shard_map.46), channel_id=1, source_target_pairs={{0,4},{4,0},{8,12},{12,8},{1,5},{5,1},{9,13},{13,9},{2,6},{6,2},{1... | collective-permute-start | bytes 73736 | tf_op jit(solution)/shard_map/ppermute | solution.py:225
  41.9 1.9 %collective-permute-done.3 = f32[48,128]{1,0:T(8,128)S(1)} collective-permute-done((f32[48,128]{1,0:T(8,128)S(1)}, f32[48,128]{1,0:T(8,128)S(1)}, u32[]{:S(2)}, u32[]{:S(2)}) %collective-permute-start.3) | collective-permute-done | bytes 24608 | tf_op jit(solution)/shard_map/ppermute | solution.py:225
  43.9 2.0 %collective-permute-start.4 = (f32[48,128]{1,0:T(8,128)S(1)}, f32[48,128]{1,0:T(8,128)S(1)}, u32[]{:S(2)}, u32[]{:S(2)}) collective-permute-start(f32[48,128]{1,0:T(8,128)S(1)} %add.36), channel_id=1, source_target_pairs={{0,8},{4,12},{8,0},{12,4},{1,9},{5,13},{9,1},{13,5},{2,10},{6,14},... | collective-permute-start | bytes 73736 | tf_op jit(solution)/shard_map/ppermute | solution.py:225
  45.8 3.7 %maxima_0_48.1.refs_0_ = f32[80,1024]{1,0:T(8,128)S(1)} custom-call(s32[512]{0:T(512)S(1)} %get-tuple-element.17.refs_0_, bf16[1024,128]{1,0:T(8,128)(2,1)S(1)} %get-tuple-element.18.refs_1_, bf16[128,64,128]{2,1,0:T(8,128)(2,1)S(1)} %get-tuple-element.22.refs_2_), custom_call_target="tpu_custom_call" | custom-call | flops 2684354560 | bytes 1638400 | tf_op jit(solution)/shard_map/maxima_0_48/pallas_call | solution.py:172
  49.5 0.0 collective-permute-done.4
  49.5 0.0 collective-permute-done.5.refs_1_
  49.6 4.6 %collective-permute-done.7.refs_2_ = f32[80,1024]{1,0:T(8,128)S(1)} collective-permute-done((f32[80,1024]{1,0:T(8,128)S(1)}, f32[80,1024]{1,0:T(8,128)S(1)}, u32[]{:S(2)}, u32[]{:S(2)}) %collective-permute-start.7) | collective-permute-done | bytes 327712 | tf_op jit(solution)/shard_map/ppermute | solution.py:225
  54.2 0.4 shard_map.47
  54.6 2.5 %collective-permute-start.10 = (f32[80,128]{1,0:T(8,128)S(1)}, f32[80,128]{1,0:T(8,128)S(1)}, u32[]{:S(2)}, u32[]{:S(2)}) collective-permute-start(f32[80,128]{1,0:T(8,128)S(1)} %shard_map.47), channel_id=1, source_target_pairs={{0,12},{4,8},{8,4},{12,0},{1,13},{5,9},{9,5},{13,1},{2,14},{6,10},... | collective-permute-start | bytes 122888 | tf_op jit(solution)/shard_map/ppermute | solution.py:225
  57.1 0.5 collective-permute-start.9
  57.6 0.5 collective-permute-start.8
  58.2 1.4 %collective-permute-done.10 = f32[80,128]{1,0:T(8,128)S(1)} collective-permute-done((f32[80,128]{1,0:T(8,128)S(1)}, f32[80,128]{1,0:T(8,128)S(1)}, u32[]{:S(2)}, u32[]{:S(2)}) %collective-permute-start.10) | collective-permute-done | bytes 40992 | tf_op jit(solution)/shard_map/ppermute | solution.py:225
  59.6 1.6 %collective-permute-done.9 = f32[80,128]{1,0:T(8,128)S(1)} collective-permute-done((f32[80,128]{1,0:T(8,128)S(1)}, f32[80,128]{1,0:T(8,128)S(1)}, u32[]{:S(2)}, u32[]{:S(2)}) %collective-permute-start.9) | collective-permute-done | bytes 40992 | tf_op jit(solution)/shard_map/ppermute | solution.py:225
  61.1 0.5 collective-permute-done.8
  61.7 0.1 collective-permute-start.11
  61.8 1.1 %collective-permute-done.11 = f32[2,128]{1,0:T(2,128)S(1)} collective-permute-done((f32[2,128]{1,0:T(2,128)S(1)}, f32[2,128]{1,0:T(2,128)S(1)}, u32[]{:S(2)}, u32[]{:S(2)}) %collective-permute-start.11) | collective-permute-done | bytes 1056 | tf_op jit(solution)/shard_map/ppermute | solution.py:225
  63.0 1.9 %collective-permute-start.14 = (f32[2,128]{1,0:T(2,128)S(1)}, f32[2,128]{1,0:T(2,128)S(1)}, u32[]{:S(2)}, u32[]{:S(2)}) collective-permute-start(f32[2,128]{1,0:T(2,128)S(1)} %pad_maximum_fusion.2), channel_id=1, source_target_pairs={{0,3},{1,2},{2,1},{3,0},{4,7},{5,6},{6,5},{7,4},{8,11},{9,10},{10,... | collective-permute-start | bytes 3080 | tf_op jit(solution)/shard_map/ppermute | solution.py:225
  64.9 0.0 collective-permute-start.13
  64.9 2.5 %collective-permute-start.12 = (f32[2,128]{1,0:T(2,128)S(1)}, f32[2,128]{1,0:T(2,128)S(1)}, u32[]{:S(2)}, u32[]{:S(2)}) collective-permute-start(f32[2,128]{1,0:T(2,128)S(1)} %pad_maximum_fusion.2), channel_id=1, source_target_pairs={{0,1},{1,0},{2,3},{3,2},{4,5},{5,4},{6,7},{7,6},{8,9},{9,8},{10,11... | collective-permute-start | bytes 3080 | tf_op jit(solution)/shard_map/ppermute | solution.py:225
  67.4 1.0 %collective-permute-done.14 = f32[2,128]{1,0:T(2,128)S(1)} collective-permute-done((f32[2,128]{1,0:T(2,128)S(1)}, f32[2,128]{1,0:T(2,128)S(1)}, u32[]{:S(2)}, u32[]{:S(2)}) %collective-permute-start.14) | collective-permute-done | bytes 1056 | tf_op jit(solution)/shard_map/ppermute | solution.py:225
  68.4 1.0 %collective-permute-done.13 = f32[2,128]{1,0:T(2,128)S(1)} collective-permute-done((f32[2,128]{1,0:T(2,128)S(1)}, f32[2,128]{1,0:T(2,128)S(1)}, u32[]{:S(2)}, u32[]{:S(2)}) %collective-permute-start.13) | collective-permute-done | bytes 1056 | tf_op jit(solution)/shard_map/ppermute | solution.py:225
  69.4 0.0 collective-permute-done.12
  69.4 0.7 %copy.5 = f32[128,128]{1,0:T(8,128)} copy(f32[128,128]{0,1:T(8,128)S(1)} %subtract_bitcast_fusion) | data formatting | bytes 131072 | tf_op jit(solution)/shard_map/transpose | solution.py:286
  (13 shorter events, 0.3 us)
Async XLA Ops:
  3.9 17.7 %collective-permute-start.1 = (f32[48,1024]{1,0:T(8,128)S(1)}, f32[48,1024]{1,0:T(8,128)S(1)}, u32[]{:S(2)}, u32[]{:S(2)}) collective-permute-start(f32[48,1024]{1,0:T(8,128)S(1)} %get-tuple-element.25), channel_id=1, source_target_pairs={{0,1},{1,0},{2,3},{3,2},{4,5},{5,4},{6,7},{7,6},{8,9},{9,8},{10,11... | collective-permute-start | bytes 589832 | tf_op jit(solution)/shard_map/ppermute | solution.py:225
  15.9 22.1 %collective-permute-start = (f32[48,1024]{1,0:T(8,128)S(1)}, f32[48,1024]{1,0:T(8,128)S(1)}, u32[]{:S(2)}, u32[]{:S(2)}) collective-permute-start(f32[48,1024]{1,0:T(8,128)S(1)} %get-tuple-element.23), channel_id=1, source_target_pairs={{0,1},{1,0},{2,3},{3,2},{4,5},{5,4},{6,7},{7,6},{8,9},{9,8},{10,11... | collective-permute-start | bytes 589832 | tf_op jit(solution)/shard_map/ppermute | solution.py:225
  16.0 19.0 %collective-permute-start.6 = (f32[80,1024]{1,0:T(8,128)S(1)}, f32[80,1024]{1,0:T(8,128)S(1)}, u32[]{:S(2)}, u32[]{:S(2)}) collective-permute-start(f32[80,1024]{1,0:T(8,128)S(1)} %get-tuple-element.27), channel_id=1, source_target_pairs={{0,1},{1,0},{2,3},{3,2},{4,5},{5,4},{6,7},{7,6},{8,9},{9,8},{10,11... | collective-permute-start | bytes 983048 | tf_op jit(solution)/shard_map/ppermute | solution.py:225
  21.5 28.1 %collective-permute-start.5 = (f32[80,1024]{1,0:T(8,128)S(1)}, f32[80,1024]{1,0:T(8,128)S(1)}, u32[]{:S(2)}, u32[]{:S(2)}) collective-permute-start(f32[80,1024]{1,0:T(8,128)S(1)} %maxima_1_48.1), channel_id=1, source_target_pairs={{0,1},{1,0},{2,3},{3,2},{4,5},{5,4},{6,7},{7,6},{8,9},{9,8},{10,11... | collective-permute-start | bytes 983048 | tf_op jit(solution)/shard_map/ppermute | solution.py:225
  21.7 17.9 %collective-permute-start.2 = (f32[48,1024]{1,0:T(8,128)S(1)}, f32[48,1024]{1,0:T(8,128)S(1)}, u32[]{:S(2)}, u32[]{:S(2)}) collective-permute-start(f32[48,1024]{1,0:T(8,128)S(1)} %max.24), channel_id=1, source_target_pairs={{0,2},{1,3},{2,0},{3,1},{4,6},{5,7},{6,4},{7,5},{8,10},{9,11},{10,... | collective-permute-start | bytes 589832 | tf_op jit(solution)/shard_map/ppermute | solution.py:225
  35.1 19.1 %collective-permute-start.7 = (f32[80,1024]{1,0:T(8,128)S(1)}, f32[80,1024]{1,0:T(8,128)S(1)}, u32[]{:S(2)}, u32[]{:S(2)}) collective-permute-start(f32[80,1024]{1,0:T(8,128)S(1)} %max.25), channel_id=1, source_target_pairs={{0,2},{1,3},{2,0},{3,1},{4,6},{5,7},{6,4},{7,5},{8,10},{9,11},{10,... | collective-permute-start | bytes 983048 | tf_op jit(solution)/shard_map/ppermute | solution.py:225
  35.7 3.9 %copy-start = (s32[128]{0:T(128)S(1)}, s32[128]{0:T(128)}, u32[]{:S(2)}) copy-start(s32[128]{0:T(128)} %param.7) | copy-start | bytes 1540
  40.0 3.9 %collective-permute-start.3 = (f32[48,128]{1,0:T(8,128)S(1)}, f32[48,128]{1,0:T(8,128)S(1)}, u32[]{:S(2)}, u32[]{:S(2)}) collective-permute-start(f32[48,128]{1,0:T(8,128)S(1)} %shard_map.46), channel_id=1, source_target_pairs={{0,4},{4,0},{8,12},{12,8},{1,5},{5,1},{9,13},{13,9},{2,6},{6,2},{1... | collective-permute-start | bytes 73736 | tf_op jit(solution)/shard_map/ppermute | solution.py:225
  43.9 5.7 %collective-permute-start.4 = (f32[48,128]{1,0:T(8,128)S(1)}, f32[48,128]{1,0:T(8,128)S(1)}, u32[]{:S(2)}, u32[]{:S(2)}) collective-permute-start(f32[48,128]{1,0:T(8,128)S(1)} %add.36), channel_id=1, source_target_pairs={{0,8},{4,12},{8,0},{12,4},{1,9},{5,13},{9,1},{13,5},{2,10},{6,14},... | collective-permute-start | bytes 73736 | tf_op jit(solution)/shard_map/ppermute | solution.py:225
  54.6 5.0 %collective-permute-start.10 = (f32[80,128]{1,0:T(8,128)S(1)}, f32[80,128]{1,0:T(8,128)S(1)}, u32[]{:S(2)}, u32[]{:S(2)}) collective-permute-start(f32[80,128]{1,0:T(8,128)S(1)} %shard_map.47), channel_id=1, source_target_pairs={{0,12},{4,8},{8,4},{12,0},{1,13},{5,9},{9,5},{13,1},{2,14},{6,10},... | collective-permute-start | bytes 122888 | tf_op jit(solution)/shard_map/ppermute | solution.py:225
  57.1 4.0 %collective-permute-start.9 = (f32[80,128]{1,0:T(8,128)S(1)}, f32[80,128]{1,0:T(8,128)S(1)}, u32[]{:S(2)}, u32[]{:S(2)}) collective-permute-start(f32[80,128]{1,0:T(8,128)S(1)} %shard_map.47), channel_id=1, source_target_pairs={{0,8},{4,12},{8,0},{12,4},{1,9},{5,13},{9,1},{13,5},{2,10},{6,14},... | collective-permute-start | bytes 122888 | tf_op jit(solution)/shard_map/ppermute | solution.py:225
  57.6 4.0 %collective-permute-start.8 = (f32[80,128]{1,0:T(8,128)S(1)}, f32[80,128]{1,0:T(8,128)S(1)}, u32[]{:S(2)}, u32[]{:S(2)}) collective-permute-start(f32[80,128]{1,0:T(8,128)S(1)} %shard_map.47), channel_id=1, source_target_pairs={{0,4},{4,0},{8,12},{12,8},{1,5},{5,1},{9,13},{13,9},{2,6},{6,2},{1... | collective-permute-start | bytes 122888 | tf_op jit(solution)/shard_map/ppermute | solution.py:225
  61.7 1.2 %collective-permute-start.11 = (f32[2,128]{1,0:T(2,128)S(1)}, f32[2,128]{1,0:T(2,128)S(1)}, u32[]{:S(2)}, u32[]{:S(2)}) collective-permute-start(f32[2,128]{1,0:T(2,128)S(1)} %pad_maximum_fusion.1), channel_id=1, source_target_pairs={{0,16},{16,0},{1,17},{17,1},{2,18},{18,2},{3,19},{19,3},{4,20},{20... | collective-permute-start | bytes 3080 | tf_op jit(solution)/shard_map/ppermute | solution.py:225
  63.0 5.4 %collective-permute-start.14 = (f32[2,128]{1,0:T(2,128)S(1)}, f32[2,128]{1,0:T(2,128)S(1)}, u32[]{:S(2)}, u32[]{:S(2)}) collective-permute-start(f32[2,128]{1,0:T(2,128)S(1)} %pad_maximum_fusion.2), channel_id=1, source_target_pairs={{0,3},{1,2},{2,1},{3,0},{4,7},{5,6},{6,5},{7,4},{8,11},{9,10},{10,... | collective-permute-start | bytes 3080 | tf_op jit(solution)/shard_map/ppermute | solution.py:225
  64.9 4.5 %collective-permute-start.13 = (f32[2,128]{1,0:T(2,128)S(1)}, f32[2,128]{1,0:T(2,128)S(1)}, u32[]{:S(2)}, u32[]{:S(2)}) collective-permute-start(f32[2,128]{1,0:T(2,128)S(1)} %pad_maximum_fusion.2), channel_id=1, source_target_pairs={{0,2},{1,3},{2,0},{3,1},{4,6},{5,7},{6,4},{7,5},{8,10},{9,11},{10,... | collective-permute-start | bytes 3080 | tf_op jit(solution)/shard_map/ppermute | solution.py:225
  64.9 4.5 %collective-permute-start.12 = (f32[2,128]{1,0:T(2,128)S(1)}, f32[2,128]{1,0:T(2,128)S(1)}, u32[]{:S(2)}, u32[]{:S(2)}) collective-permute-start(f32[2,128]{1,0:T(2,128)S(1)} %pad_maximum_fusion.2), channel_id=1, source_target_pairs={{0,1},{1,0},{2,3},{3,2},{4,5},{5,4},{6,7},{7,6},{8,9},{9,8},{10,11... | collective-permute-start | bytes 3080 | tf_op jit(solution)/shard_map/ppermute | solution.py:225
